TPU v7x, 32 devices: a whole 2x2x4 slice. The times are simulated.
32 devices in a mesh: pts: 16 (over z, y, x), cand: 2 (over core).
Axes of the slice: x: 2, y: 2, z: 4, core: 2. Of those that a mesh axis runs over, the one named last changes fastest.
Arguments:
- points: bfloat16 [8192, 4096], P('pts'), may hold values from -6 to 6
- weights: float32 [8192], P('pts'), may hold values from 0.25 to 4
- coverage: float32 [8192], P('pts'), may hold values from 0 to 1.5
- cand_index: int32 [2, 256], P(None, 'pts'), may hold values from 0 to 511
- winners: int32 [2], replicated, may hold values from 0 to 255
Outputs:
- gains: float32 [2, 256], P(None, ('pts', 'cand'))
- final_cover: float32 [8192], P('pts')
All inputs are finite; a program needn't handle non-finite values.
Results may differ from a plain program's by a relative error of at most 0.0003.
Values may be sent and summed in bfloat16 or wider, within the bound.
A program may use at most 64 MiB of HBM per device.

v0:
```python
import jax
import jax.numpy as jnp
from jax import lax
from jax.sharding import PartitionSpec as P


def broadcast(array, axis, root):
    mine = lax.axis_index(axis) == root
    return lax.psum(jnp.where(mine, array, jnp.zeros_like(array)), axis)


def gain_terms(points, rows, weights, cover, scale, total):
    sim = (
        lax.dot_general(points, rows, (((1,), (1,)), ((), ())), preferred_element_type=jnp.float32)
        * scale
    )
    return jnp.sum(weights[:, None] * jnp.maximum(sim - cover[:, None], 0.0), axis=0) / total


def body(points, weights, coverage, cand_index, winners):
    rows_dev = points.shape[0]
    width = points.shape[1]
    n_pts = lax.axis_size("pts")
    n_cand = lax.axis_size("cand")
    per_row = cand_index.shape[1]
    per_dev = per_row // n_cand
    total = float(rows_dev * n_pts)
    scale = width ** (-0.5)
    my_cand = lax.axis_index("cand")
    my_pts = lax.axis_index("pts")
    mine = lax.dynamic_slice_in_dim(cand_index, my_cand * per_dev, per_dev, 1)
    cover = coverage
    results = []
    for step in range(cand_index.shape[0]):
        picked = jnp.take(points, mine[step], axis=0)
        frozen = cover
        part = gain_terms(
            points, lax.all_gather(picked, "pts", axis=0, tiled=True), weights, frozen, scale, total
        )
        results.append(lax.psum(part, "pts"))
        column = winners[step]
        owner_pts = column // per_row
        offset = jnp.clip(column - my_pts * per_row, 0, per_row - 1)
        point_row = cand_index[step][offset]
        local = lax.dynamic_slice_in_dim(points, point_row, 1, 0)
        chosen = broadcast(local, "pts", owner_pts)
        sim = (
            lax.dot_general(
                points, chosen, (((1,), (1,)), ((), ())), preferred_element_type=jnp.float32
            )[:, 0]
            * scale
        )
        cover = jnp.maximum(cover, sim)
    summed = jnp.stack(results)
    gains = lax.dynamic_slice_in_dim(summed, my_pts * per_dev, per_dev, 1)
    return (gains, cover)


def solution(mesh):
    placed = (P("pts", None), P("pts"), P("pts"), P(None, "pts"), P())
    return jax.shard_map(
        body,
        mesh=mesh,
        in_specs=placed,
        out_specs=(P(None, ("pts", "cand")), P("pts")),
        check_vma=False,
    )
```

profile of v0, /device:TPU:0, one launch (start us, length us, event | category | flops | bytes accessed | tf_op | source)
XLA Modules:
  0.0 178.4 jit_solution(8794232108676989060)
XLA Ops:
  7.2 0.0 all-gather.5.cloned.1.call-start
  7.2 0.8 constant_dynamic-slice_fusion.3
  8.0 3.4 %gather_fusion.1 = bf16[8,4096]{1,0:T(8,128)(2,1)S(1)} fusion(bf16[512,4096]{1,0:T(8,128)(2,1)} %param.7, s32[1024]{0:T(1024)S(1)} %pad_clamp_fusion), kind=kCustom, calls=%fused_computation.1.clone | custom fusion | bytes 131104 | tf_op jit(solution)/shard_map/jit(_take)/gather | solution.py:35
  11.4 0.7 broadcast_select_fusion
  12.1 0.0 all-gather.5.cloned.1.call-update
  12.1 0.0 all-gather.3.cloned.1.call-start
  12.2 3.4 %gather_fusion = bf16[8,4096]{1,0:T(8,128)(2,1)S(1)} fusion(bf16[512,4096]{1,0:T(8,128)(2,1)} %param.7, s32[1024]{0:T(1024)S(1)} %pad_clamp_fusion.1), kind=kCustom, calls=%fused_computation.clone | custom fusion | bytes 131104 | tf_op jit(solution)/shard_map/jit(_take)/gather | solution.py:35
  15.5 0.7 broadcast_select_fusion.1
  16.2 0.0 all-gather.3.cloned.1.call-update
  16.3 1.3 fusion.11
  20.8 0.8 fusion.10
  21.6 0.7 constant_dynamic-slice_fusion
  29.5 1.0 fusion.9
  30.5 78.9 %all-reduce.1 = (bf16[4096]{0:T(1024)(128)(2,1)S(1)}, bf16[4096]{0:T(1024)(128)(2,1)S(1)}) all-reduce(bf16[4096]{0:T(1024)(128)(2,1)S(1)} %get-tuple-element.4, bf16[4096]{0:T(1024)(128)(2,1)S(1)} %get-tuple-element.3), channel_id=1, replica_groups=mesh['pts'=16,'cand'=2] {'pts'}, use_global_device_ids=true, to_apply=%region_2.4 | all-reduce | flops 8192 | bytes 32768 | tf_op jit(solution)/shard_map/psum | solution.py:9
  109.4 0.0 copy-start
  109.4 0.0 copy-start.2
  109.4 0.0 copy-start.1
  109.4 3.5 %fusion.13 = f32[1,512]{1,0:T(1,128)S(1)} fusion(bf16[4096,1]{0,1:T(2,128)(2,1)S(1)} %reshape.52, bf16[512,4096]{1,0:T(8,128)(2,1)} %param.7), kind=kOutput, calls=%fused_computation.36 | convolution fusion | flops 4194304 | bytes 4204544 | tf_op jit(solution)/shard_map/dot_general | solution.py:48
  113.0 0.0 copy-done
  113.0 1.2 fusion.12
  114.2 0.0 copy-done.2
  114.2 0.6 multiply_maximum_fusion
  114.8 0.0 all-gather.5.cloned.1.call-done
  114.8 0.0 copy-done.1
  114.8 4.1 %fusion.7 = f32[128]{0:T(128)S(1)} fusion(bf16[128,4096]{1,0:T(8,128)(2,1)} %all-gather.5.cloned.1.call-done, bf16[512,4096]{1,0:T(8,128)(2,1)} %param.7, f32[512]{0:T(512)S(1)} %get-tuple-element.10, f32[512]{0:T(512)S(1)} %copy-done.1), kind=kOutput, calls=%fused_computation.11 | convolution fusion | flops 537198464 | bytes 5247488 | tf_op jit(solution)/shard_map/dot_general | solution.py:14
  118.9 8.2 %all-gather.3.cloned.1.call-done = bf16[128,4096]{1,0:T(8,128)(2,1)} async-done(((bf16[8,4096]{1,0:T(8,128)(2,1)}), bf16[128,4096]{1,0:T(8,128)(2,1)}) %all-gather.3.cloned.1.call-update) | async-done | bytes 1048592 | tf_op jit(solution)/shard_map/all_gather | solution.py:38
  127.1 4.1 %fusion.6 = f32[128]{0:T(128)S(1)} fusion(bf16[128,4096]{1,0:T(8,128)(2,1)} %all-gather.3.cloned.1.call-done, bf16[512,4096]{1,0:T(8,128)(2,1)} %param.7, f32[512]{0:T(512)S(1)} %copy-done.2, f32[512]{0:T(512)S(1)} %copy-done.1), kind=kOutput, calls=%fused_computation.10 | convolution fusion | flops 537198464 | bytes 5247488 | tf_op jit(solution)/shard_map/dot_general | solution.py:14
  131.3 39.6 %all-reduce = (f32[1,128]{1,0:T(1,128)S(1)}, f32[1,128]{1,0:T(1,128)S(1)}) all-reduce(f32[1,128]{1,0:T(1,128)S(1)} %multiply_bitcast_fusion, f32[1,128]{1,0:T(1,128)S(1)} %multiply_bitcast_fusion.1), channel_id=1, replica_groups=mesh['pts'=16,'cand'=2] {'pts'}, use_global_device_ids=true, to_apply=%region_4.6 | all-reduce | flops 256 | bytes 2048 | tf_op jit(solution)/shard_map/psum | solution.py:40
  170.9 0.6 constant_dynamic-slice_fusion.1
  (8 shorter events, 0.1 us)
Async XLA Ops:
  7.2 107.6 %all-gather.5.cloned.1.call-start = ((), (), s32[]{:S(2)}) async-start(), calls=%async_computation.1 | async-start | bytes 1114112 | tf_op jit(solution)/shard_map/all_gather | solution.py:38
  12.1 115.0 %all-gather.3.cloned.1.call-start = ((), (), s32[]{:S(2)}) async-start(), calls=%async_computation | async-start | bytes 1114112 | tf_op jit(solution)/shard_map/all_gather | solution.py:38
  109.4 3.6 %copy-start = (bf16[512,4096]{1,0:T(8,128)(2,1)S(1)}, bf16[512,4096]{1,0:T(8,128)(2,1)}, u32[]{:S(2)}) copy-start(bf16[512,4096]{1,0:T(8,128)(2,1)} %param.7) | copy-start | bytes 12582916
  109.4 4.7 %copy-start.2 = (f32[512]{0:T(512)S(1)}, f32[512]{0:T(512)}, u32[]{:S(2)}) copy-start(f32[512]{0:T(512)} %param.9) | copy-start | bytes 6148
  109.4 5.3 %copy-start.1 = (f32[512]{0:T(512)S(1)}, f32[512]{0:T(512)}, u32[]{:S(2)}) copy-start(f32[512]{0:T(512)} %param.8) | copy-start | bytes 6148
Sparse Core Ops, SparseCore 0:
  12.2 58.1 all-gather.4
  73.2 53.9 all-gather.2
where the time goes:
time: 179 us; the launch traced here: 178 us
  blocking collectives  119 us (66%)
  between operations  24.6 us (14%)
  matrix products  13 us (7%)
  local copies, waits for them, and re-layouts  10.9 us (6%)
  waiting for transfers between devices  8.27 us (5%)
  other arithmetic  3.02 us (2%)
    psum x1, blocking collectives, broadcast(): return lax.psum(jnp.where(mine, array, jnp.zeros_like(array)), axis)  78.9 us
    psum x1, blocking collectives, body(): results.append(lax.psum(part, 'pts'))  39.6 us
    dot_general x2, matrix products, gain_terms(): lax.dot_general(points, rows, (((1,), (1,)), ((), ())), preferred_element...  8.26 us
    all_gather x2, waiting for transfers between devices, body(): lax.all_gather(picked, 'pts', axis=0, tiled=True)  8.24 us
    gather x2, local copies, waits for them, and re-layouts, body(): picked = jnp.take(points, mine[step], axis=0)  6.75 us
    dot_general x2, matrix products, body(): lax.dot_general(points, chosen, (((1,), (1,)), ((), ())), preferred_eleme...  4.71 us
  transfers between devices with their start and end apart: 2, of which 1 were waited for; matrix products, arithmetic and copies ran while one was open for 10% of the time, Pallas kernels for 0%

commit v1 on v0

v1 whole, which is shorter than its diff:
```python
import functools

import jax
import jax.numpy as jnp
from jax import lax
from jax.experimental import pallas as pl
from jax.experimental.pallas import tpu as pltpu
from jax.sharding import PartitionSpec as P

MESH = pl.DeviceIdType.MESH
CHUNKS = 4


def kernel(n, m, iters, per_dev, points_hbm, weight_ref, cover_ref, index_ref, winner_ref,
           gains_ref, final_ref, points, cands, sims, cols, parts, padded,
           load_sem, send_sem, recv_sem, col_send, col_recv, part_send, part_recv):
    me = lax.axis_index("pts")
    mine = lax.axis_index("cand")
    length = n // 4
    z = me // 4
    lane = me % 4
    x, y = lane % 2, lane // 2
    rows, width = points.shape
    block = iters * per_dev
    step_cols = width // CHUNKS
    scale = width ** (-0.5)

    load = pltpu.make_async_copy(points_hbm, points, load_sem)
    load.start()

    to_x = z * 4 + y * 2 + (1 - x)
    to_y = z * 4 + (1 - y) * 2 + x
    up, down = me + 4, me - 4
    has_up, has_down = z < length - 1, z > 0

    barrier = pltpu.get_barrier_semaphore()

    def greet(pts, cand):
        pl.semaphore_signal(barrier, inc=1, device_id=(pts, cand), device_id_type=MESH)

    greet(to_x, mine)
    greet(to_y, mine)
    for other in range(1, m):
        greet(me, lax.rem(mine + other, m))
    pl.when(has_up)(lambda: greet(up, mine))
    pl.when(has_down)(lambda: greet(down, mine))

    load.wait()
    place_row = lax.broadcasted_iota(jnp.int32, (block, rows), 0)
    place_col = lax.broadcasted_iota(jnp.int32, (block, rows), 1)
    choose = jnp.zeros((block, rows), jnp.float32)
    for t in range(iters):
        for k in range(per_dev):
            hit = place_col == index_ref[t, mine * per_dev + k]
            choose = jnp.where((place_row == t * per_dev + k) & hit, 1.0, choose)
    choose = choose.astype(jnp.bfloat16)
    for q in range(CHUNKS):
        span = slice(q * step_cols, (q + 1) * step_cols)
        cands[me, :, span] = jnp.dot(
            choose, points[:, span], preferred_element_type=jnp.float32).astype(jnp.bfloat16)

    pl.semaphore_wait(
        barrier, 2 + (m - 1) + has_up.astype(jnp.int32) + has_down.astype(jnp.int32))

    def columns(q):
        return pl.ds(pl.multiple_of(q * step_cols, 128), step_cols)

    def copy(p, q, way, target):
        part = cands.at[p, :, columns(q)]
        return pltpu.make_async_remote_copy(
            src_ref=part, dst_ref=part, send_sem=send_sem.at[p, way],
            recv_sem=recv_sem.at[p, q], device_id=(target, mine), device_id_type=MESH)

    last = length - 1
    is_end = (z == 0) | (z == last)

    def direct(zp):
        outer = (zp == 0) | (zp == last)
        return outer == is_end

    def routes(kind, zp):
        if kind == 0:
            return [(2, has_up & (zp <= z), up), (3, has_down & (zp >= z), down),
                    (0, None, to_x), (1, None, to_y)]
        if kind == 1:
            return [(1, direct(zp) & (zp % 2 == 1), to_y)]
        if kind == 2:
            return [(0, direct(zp) & (zp % 2 == 0), to_x)]
        inner = (zp > 0) & (zp < last)
        return [(2, (inner & (z == last - 1)) | ((zp == 0) & (z < last - 1)), up),
                (3, (inner & (z == 1)) | ((zp == last) & (z > 1)), down)]

    lanes = [lane, y * 2 + (1 - x), (1 - y) * 2 + x, (1 - y) * 2 + (1 - x)]

    def forward(kind, zp, q):
        p = zp * 4 + lanes[kind]
        for way, wanted, target in routes(kind, zp):
            def go(way=way, target=target):
                copy(p, q, way, target).start()
            if wanted is None:
                go()
            else:
                pl.when(wanted)(go)

    def settle(kind, zp):
        p = zp * 4 + lanes[kind]
        for way, wanted, target in routes(kind, zp):
            def go(way=way, target=target):
                pltpu.make_async_remote_copy(
                    src_ref=cands.at[p], dst_ref=cands.at[p], send_sem=send_sem.at[p, way],
                    recv_sem=recv_sem.at[p, 0], device_id=(target, mine),
                    device_id_type=MESH).wait_send()
            if wanted is None:
                go()
            else:
                pl.when(wanted)(go)

    for q in range(CHUNKS):
        forward(0, z, q)

    def stage(s, q):
        for kind, delay in ((3, 2), (0, 0), (1, 1), (2, 1)):
            for sign in (-1, 1):
                d = s - delay
                zp = z + sign * d
                valid = (zp >= 0) & (zp <= last) & (d >= (1 if kind == 0 or sign == 1 else 0))

                @pl.when(valid)
                def _(kind=kind, zp=zp):
                    copy(zp * 4 + lanes[kind], q, 0, to_x).wait_recv()
                    forward(kind, zp, q)

    def all_chunks(s, carry):
        lax.fori_loop(0, CHUNKS, lambda q, c: (stage(s, q), c)[1], 0)
        return carry

    lax.fori_loop(1, length + 1, all_chunks, 0)
    for q in range(CHUNKS):
        stage(length + 1, q)
        span = slice(q * step_cols, (q + 1) * step_cols)
        product = lax.dot_general(
            cands[:, :, span].reshape(n * block, step_cols), points[:, span],
            (((1,), (1,)), ((), ())), preferred_element_type=jnp.float32)
        if q == 0:
            sims[...] = product
        elif q < CHUNKS - 1:
            sims[...] += product
        else:
            sims[...] = (sims[...] + product) * scale

    def sim_of(t):
        return sims[...].reshape(n, iters, per_dev, rows)[:, t].reshape(n * per_dev, rows)

    place = lax.broadcasted_iota(jnp.int32, (n * per_dev, 1), 0)
    column = (place // per_dev) * (per_dev * m) + mine * per_dev + place % per_dev
    for t in range(iters):
        picked = jnp.where(column == winner_ref[t], sim_of(t), 0.0)
        cols[mine, t:t + 1, :] = jnp.sum(picked, axis=0, keepdims=True)

    def col_copy(slot, peer):
        return pltpu.make_async_remote_copy(
            src_ref=cols.at[slot], dst_ref=cols.at[slot], send_sem=col_send.at[peer],
            recv_sem=col_recv.at[slot], device_id=(me, peer), device_id_type=MESH)

    peers = [lax.rem(mine + other, m) for other in range(1, m)]
    for peer in peers:
        col_copy(mine, peer).start()

    weight = weight_ref[...]

    def gain(t, cover):
        terms = weight * jnp.maximum(sim_of(t) - cover, 0.0)
        folded = terms[:, 0:128]
        for g in range(1, rows // 128):
            folded = folded + terms[:, g * 128:(g + 1) * 128]
        return jnp.sum(folded.T, axis=0, keepdims=True)

    cover = cover_ref[...]
    for t in range(iters):
        parts[me, t:t + 1, :] = gain(t, cover)
        if t == 0:
            for peer in peers:
                col_copy(peer, peer).wait_recv()
        best = cols[0, t:t + 1, :]
        for c in range(1, m):
            best = best + cols[c, t:t + 1, :]
        cover = jnp.maximum(cover, best)

    def part_copy(slot, target):
        return pltpu.make_async_remote_copy(
            src_ref=parts.at[slot], dst_ref=parts.at[slot], send_sem=part_send.at[target],
            recv_sem=part_recv.at[slot], device_id=(target, mine), device_id_type=MESH)

    others = [lax.rem(me + other, n) for other in range(1, n)]
    for target in others:
        part_copy(me, target).start()
    final_ref[...] = cover

    settle(0, z)
    for kind in range(4):
        def each(zp, carry, kind=kind):
            if kind == 0:
                pl.when(zp != z)(lambda: settle(0, zp))
            else:
                settle(kind, zp)
            return carry
        lax.fori_loop(0, length, each, 0)
    for peer in peers:
        col_copy(mine, peer).wait_send()

    for source in others:
        part_copy(source, source).wait_recv()
    total = parts[0]
    for p in range(1, n):
        total = total + parts[p]
    padded[...] = jnp.zeros_like(padded)
    padded[0:iters, :] = total / float(rows * n)
    turned = pltpu.roll(padded[...], (n - me) * per_dev, 1)
    gains_ref[...] = turned[0:iters, 0:per_dev]
    for target in others:
        part_copy(me, target).wait_send()


def solution(mesh):
    n, m = mesh.shape["pts"], mesh.shape["cand"]

    def body(points, weights, coverage, cand_index, winners):
        rows, width = points.shape
        iters, per_row = cand_index.shape
        per_dev = per_row // m
        block = iters * per_dev
        vmem = pl.BlockSpec(memory_space=pltpu.VMEM)
        smem = pl.BlockSpec(memory_space=pltpu.SMEM)
        dma = pltpu.SemaphoreType.DMA
        gains, final = pl.pallas_call(
            functools.partial(kernel, n, m, iters, per_dev),
            out_shape=(jax.ShapeDtypeStruct((iters, per_dev), jnp.float32),
                       jax.ShapeDtypeStruct((1, rows), jnp.float32)),
            in_specs=[pl.BlockSpec(memory_space=pl.ANY), vmem, vmem, smem, smem],
            out_specs=(vmem, vmem),
            scratch_shapes=[
                pltpu.VMEM((rows, width), jnp.bfloat16),
                pltpu.VMEM((n, block, width), jnp.bfloat16),
                pltpu.VMEM((n * block, rows), jnp.float32),
                pltpu.VMEM((m, iters, rows), jnp.float32),
                pltpu.VMEM((n, iters, n * per_dev), jnp.float32),
                pltpu.VMEM((8, n * per_dev), jnp.float32),
                dma, dma((n, 4)), dma((n, CHUNKS)), dma((m,)), dma((m,)), dma((n,)), dma((n,)),
            ],
            compiler_params=pltpu.CompilerParams(collective_id=0, has_side_effects=True),
        )(points, weights.reshape(1, rows), coverage.reshape(1, rows), cand_index, winners)
        return gains, final.reshape(rows)

    return jax.shard_map(
        body,
        mesh=mesh,
        in_specs=(P("pts", None), P("pts"), P("pts"), P(None, "pts"), P()),
        out_specs=(P(None, ("pts", "cand")), P("pts")),
        check_vma=False,
    )
```

time: 179 us -> 40.9 us (0.23)
  blocking collectives: 119 us -> 0 us
  Pallas kernels: 0 us -> 37.5 us
  between operations: 24.6 us -> 0.64 us
  matrix products: 13 us -> 0 us
  local copies, waits for them, and re-layouts: 10.9 us -> 2.46 us
  waiting for transfers between devices: 8.27 us -> 0 us
  other arithmetic: 3.02 us -> 0 us
    psum x2 -> x0, blocking collectives: 119 us -> none  [the longest x1 78.9 us: broadcast(): return lax.psum(jnp.where(mine, array, jnp.zeros_like(array)), axis)]
    pallas_call x0 -> x1, Pallas kernels: none -> 37.5 us  [body(): pl.pallas_call(functools.partial(kernel, n, m, iters, per_dev), out_shape...]
    dot_general x4 -> x0, matrix products: 13 us -> none  [the longest x2 8.26 us: gain_terms(): lax.dot_general(points, rows, (((1,), (1,)), ((), ())), preferred_element...]
    all_gather x2 -> x0, waiting for transfers between devices: 8.24 us -> none  [body(): lax.all_gather(picked, 'pts', axis=0, tiled=True)]
    gather x2 -> x0, local copies, waits for them, and re-layouts: 6.75 us -> none  [body(): picked = jnp.take(points, mine[step], axis=0)]
    unnamed x6 -> x2, local copies, waits for them, and re-layouts: 0.02 us -> 2.46 us
    select_n x3 -> x0, other arithmetic: 2.38 us -> none  [the longest x2 1.39 us: body(): picked = jnp.take(points, mine[step], axis=0)]
    slice x2 -> x0, local copies, waits for them, and re-layouts: 2.07 us -> none  [the longest x1 1.31 us: body(): column = winners[step]]
  transfers between devices with their start and end apart: 2 -> 0, of which waited for: 1 -> 0; matrix products, arithmetic and copies ran while one was open for 10% -> 0% of each run, Pallas kernels for 0% -> 0%
where the time goes in v1:
time: 40.9 us; the launch traced here: 40.6 us
  Pallas kernels  37.5 us (92%)
  local copies, waits for them, and re-layouts  2.46 us (6%)
  between operations  0.64 us (2%)
    pallas_call x1, Pallas kernels, body(): pl.pallas_call(functools.partial(kernel, n, m, iters, per_dev), out_shape...  37.5 us
    unnamed x2, local copies, waits for them, and re-layouts  2.46 us

profile of v1, /device:TPU:0, one launch (start us, length us, event | category | flops | bytes accessed | tf_op | source)
XLA Modules:
  0.0 40.6 jit_solution(9380169636217172985)
XLA Ops:
  0.6 37.5 %shard_map.68 = (f32[2,8]{1,0:T(2,128)}, f32[1,512]{1,0:T(1,128)}) custom-call(bf16[512,4096]{1,0:T(8,128)(2,1)} %points_hbm.1, f32[1,512]{1,0:T(1,128)} %bitcast.3, f32[1,512]{1,0:T(1,128)} %bitcast.4, s32[2,16]{1,0:T(2,128)} %index_ref.1, s32[2]{0:T(128)} %winner_ref.1), custom_call_target="tpu_custom_call" | custom-call | tf_op jit(solution)/shard_map/pallas_call | solution.py:235
  38.2 1.2 %copy.9 = f32[2,8]{1,0:T(2,128)} copy(f32[2,8]{1,0:T(2,128)} %get-tuple-element.8) | data formatting | bytes 128
  39.4 1.2 %copy.10 = f32[512]{0:T(512)} copy(f32[512]{0:T(512)} %bitcast.5) | data formatting | bytes 4096

commit v2 on v1

--- a/solution.py
+++ b/solution.py
@@ -8,7 +8,7 @@
 from jax.sharding import PartitionSpec as P
 
 MESH = pl.DeviceIdType.MESH
-CHUNKS = 4
+CHUNKS = 8
 
 
 def kernel(n, m, iters, per_dev, points_hbm, weight_ref, cover_ref, index_ref, winner_ref,
@@ -72,11 +72,10 @@
             recv_sem=recv_sem.at[p, q], device_id=(target, mine), device_id_type=MESH)
 
     last = length - 1
-    is_end = (z == 0) | (z == last)
+    middle = length // 2
 
     def direct(zp):
-        outer = (zp == 0) | (zp == last)
-        return outer == is_end
+        return (zp >= middle) == (z >= middle)
 
     def routes(kind, zp):
         if kind == 0:
@@ -86,9 +85,8 @@
             return [(1, direct(zp) & (zp % 2 == 1), to_y)]
         if kind == 2:
             return [(0, direct(zp) & (zp % 2 == 0), to_x)]
-        inner = (zp > 0) & (zp < last)
-        return [(2, (inner & (z == last - 1)) | ((zp == 0) & (z < last - 1)), up),
-                (3, (inner & (z == 1)) | ((zp == last) & (z > 1)), down)]
+        return [(2, (zp < middle) & (z >= middle - 1) & has_up, up),
+                (3, (zp >= middle) & (z <= middle) & has_down, down)]
 
     lanes = [lane, y * 2 + (1 - x), (1 - y) * 2 + x, (1 - y) * 2 + (1 - x)]
 
@@ -249,6 +247,18 @@
             ],
             compiler_params=pltpu.CompilerParams(collective_id=0, has_side_effects=True),
         )(points, weights.reshape(1, rows), coverage.reshape(1, rows), cand_index, winners)
+
+        def emit(gains_in, final_in, gains_out, final_out):
+            gains_out[...] = gains_in[...]
+            final_out[...] = final_in[...]
+
+        gains, final = pl.pallas_call(
+            emit,
+            out_shape=(jax.ShapeDtypeStruct((iters, per_dev), jnp.float32),
+                       jax.ShapeDtypeStruct((1, rows), jnp.float32)),
+            in_specs=[vmem, vmem],
+            out_specs=(vmem, vmem),
+        )(gains, final)
         return gains, final.reshape(rows)
 
     return jax.shard_map(

time: 40.9 us -> 38.6 us (0.944)
  local copies, waits for them, and re-layouts: 2.46 us -> 0 us
    unnamed x2 -> x0, local copies, waits for them, and re-layouts: 2.46 us -> none
    pallas_call x0 -> x1, Pallas kernels: none -> 1.25 us  [body(): pl.pallas_call(emit, out_shape=(jax.ShapeDtypeStruct((iters, per_dev), jn...]
    pallas_call x1, Pallas kernels: 37.5 us -> 36.5 us  [body(): pl.pallas_call(functools.partial(kernel, n, m, iters, per_dev), out_shape...]
where the time goes in v2:
time: 38.6 us; the launch traced here: 38.4 us
  Pallas kernels  37.7 us (98%)
  between operations  0.64 us (2%)
    pallas_call x1, Pallas kernels, body(): pl.pallas_call(functools.partial(kernel, n, m, iters, per_dev), out_shape...  36.5 us
    pallas_call x1, Pallas kernels, body(): pl.pallas_call(emit, out_shape=(jax.ShapeDtypeStruct((iters, per_dev), jn...  1.25 us

profile of v2, /device:TPU:0, one launch (start us, length us, event | category | flops | bytes accessed | tf_op | source)
XLA Modules:
  0.0 38.4 jit_solution(1776092568719908049)
XLA Ops:
  0.6 36.5 %shard_map.68 = (f32[2,8]{1,0:T(2,128)}, f32[1,512]{1,0:T(1,128)}) custom-call(bf16[512,4096]{1,0:T(8,128)(2,1)} %points_hbm.1, f32[1,512]{1,0:T(1,128)} %bitcast.3, f32[1,512]{1,0:T(1,128)} %bitcast.4, s32[2,16]{1,0:T(2,128)} %index_ref.1, s32[2]{0:T(128)} %winner_ref.1), custom_call_target="tpu_custom_call" | custom-call | tf_op jit(solution)/shard_map/pallas_call | solution.py:233
  37.1 1.3 %shard_map.69 = (f32[2,8]{1,0:T(2,128)}, f32[1,512]{1,0:T(1,128)}) custom-call(f32[2,8]{1,0:T(2,128)} %get-tuple-element.6.gains_in, f32[1,512]{1,0:T(1,128)} %get-tuple-element.7.final_in), custom_call_target="tpu_custom_call" | custom-call | tf_op jit(solution)/shard_map/pallas_call | solution.py:255

commit v3 on v2

--- a/solution.py
+++ b/solution.py
@@ -117,7 +117,7 @@
         forward(0, z, q)
 
     def stage(s, q):
-        for kind, delay in ((3, 2), (0, 0), (1, 1), (2, 1)):
+        for kind, delay in ((0, 0), (1, 1), (2, 1), (3, 2)):
             for sign in (-1, 1):
                 d = s - delay
                 zp = z + sign * d

time: 38.6 us -> 38.2 us (0.990)
  Pallas kernels: 37.7 us -> 37.3 us
    pallas_call x1, Pallas kernels: 36.5 us -> 36.1 us  [body(): pl.pallas_call(functools.partial(kernel, n, m, iters, per_dev), out_shape...]
where the time goes in v3:
time: 38.2 us; the launch traced here: 38 us
  Pallas kernels  37.3 us (98%)
  between operations  0.64 us (2%)
    pallas_call x1, Pallas kernels, body(): pl.pallas_call(functools.partial(kernel, n, m, iters, per_dev), out_shape...  36.1 us
    pallas_call x1, Pallas kernels, body(): pl.pallas_call(emit, out_shape=(jax.ShapeDtypeStruct((iters, per_dev), jn...  1.25 us

profile of v3, /device:TPU:0, one launch (start us, length us, event | category | flops | bytes accessed | tf_op | source)
XLA Modules:
  0.0 38.0 jit_solution(17506293874886355655)
XLA Ops:
  0.6 36.1 %shard_map.68 = (f32[2,8]{1,0:T(2,128)}, f32[1,512]{1,0:T(1,128)}) custom-call(bf16[512,4096]{1,0:T(8,128)(2,1)} %points_hbm.1, f32[1,512]{1,0:T(1,128)} %bitcast.3, f32[1,512]{1,0:T(1,128)} %bitcast.4, s32[2,16]{1,0:T(2,128)} %index_ref.1, s32[2]{0:T(128)} %winner_ref.1), custom_call_target="tpu_custom_call" | custom-call | tf_op jit(solution)/shard_map/pallas_call | solution.py:233
  36.7 1.3 %shard_map.69 = (f32[2,8]{1,0:T(2,128)}, f32[1,512]{1,0:T(1,128)}) custom-call(f32[2,8]{1,0:T(2,128)} %get-tuple-element.6.gains_in, f32[1,512]{1,0:T(1,128)} %get-tuple-element.7.final_in), custom_call_target="tpu_custom_call" | custom-call | tf_op jit(solution)/shard_map/pallas_call | solution.py:255
